TPU v7x, 8 devices: a whole 2x2x1 slice. The times are simulated.
8 devices in a mesh: seqs: 1 (over z), states: 8 (over y, x, core).
Axes of the slice: x: 2, y: 2, z: 1, core: 2. Of those that a mesh axis runs over, the one named last changes fastest.
Arguments:
- trans_mat: bfloat16 [16384, 16384], P(None, 'states')
- emit_mat: bfloat16 [16384, 10000], P('states')
- init_prob: float32 [16384], P('states')
- tokens: int32 [128, 64], P('seqs')
- lengths: int32 [128], P('seqs')
Outputs:
- output 1: float32 [128], P('seqs')
- output 2: float32 [128, 16384], P('seqs', 'states')
All inputs are finite; a program needn't handle non-finite values.
Results may differ from a plain program's by a relative error of at most 0.001.
Values are sent between devices in bfloat16 or wider.
A program may use at most 1 GiB of HBM per device.

v0:
```python
import jax
import jax.numpy as jnp
from jax import lax
from jax.sharding import PartitionSpec as P


def solution(mesh):
    def local_run(trans_cols, emit_rows, init_part, token_rows, length_rows):
        num_steps = token_rows.shape[1]

        def emission(step_idx):
            token_col = lax.dynamic_index_in_dim(token_rows, step_idx, axis=1, keepdims=False)
            return jnp.take(emit_rows, token_col, axis=1).T.astype(jnp.float32)

        first_prob = init_part[None, :] * emission(0)
        first_norm = lax.psum(jnp.sum(first_prob, axis=1), "states")
        state_prob = first_prob / first_norm[:, None]
        log_lik = jnp.log(first_norm)

        def one_step(step_idx, carried):
            state_prob, log_lik = carried
            gathered = lax.all_gather(state_prob.astype(jnp.bfloat16), "states", axis=1, tiled=True)
            predicted = jnp.dot(gathered, trans_cols, preferred_element_type=jnp.float32)
            new_prob = predicted * emission(step_idx)
            step_norm = lax.psum(jnp.sum(new_prob, axis=1), "states")
            new_prob = new_prob / step_norm[:, None]
            is_live = step_idx < length_rows
            state_prob = jnp.where(is_live[:, None], new_prob, state_prob)
            log_lik = log_lik + jnp.where(is_live, jnp.log(step_norm), 0.0)
            return state_prob, log_lik

        state_prob, log_lik = lax.fori_loop(1, num_steps, one_step, (state_prob, log_lik))
        return log_lik, state_prob

    return jax.shard_map(
        local_run,
        mesh=mesh,
        in_specs=(P(None, "states"), P("states", None), P("states"), P("seqs", None), P("seqs")),
        out_specs=(P("seqs"), P("seqs", "states")),
        check_vma=False,
    )
```

profile of v0, /device:TPU:0, one launch (start us, length us, event | category | flops | bytes accessed | tf_op | source)
XLA Modules:
  0.0 5217.2 jit_solution(16085642090048280424)
XLA Ops:
  37.6 5172.1 %while.17 = (s32[]{:T(128)}, f32[128,2048]{1,0:T(8,128)S(1)}, f32[128]{0:T(128)S(1)}, s32[128]{0:T(128)}, bf16[16384,2048]{1,0:T(8,128)(2,1)}, /*index=5*/s32[12...) while((s32[]{:T(128)}, f32[128,2048]{1,0:T(8,128)S(1)}, f32[128]{0:T(128)S(1)}, ...), condition=%wide.region_5.7_spmd, body=%wide.region_2.0_spmd.sunk | while | flops 8591771648 | bytes 92811992 | solution.py:32
  123.3 31.4 all-gather.2.cloned.1.call-done
  533.7 31.4 all-gather.2.cloned.1.call-done
  615.9 31.4 all-gather.2.cloned.1.call-done
  698.2 31.4 all-gather.2.cloned.1.call-done
  1026.6 31.4 all-gather.2.cloned.1.call-done
  1518.6 31.4 all-gather.2.cloned.1.call-done
  1765.1 31.4 all-gather.2.cloned.1.call-done
  2011.5 31.4 all-gather.2.cloned.1.call-done
  2257.7 31.4 all-gather.2.cloned.1.call-done
  2340.0 31.4 all-gather.2.cloned.1.call-done
  2586.4 31.4 all-gather.2.cloned.1.call-done
  2832.9 31.4 all-gather.2.cloned.1.call-done
  3079.0 31.4 all-gather.2.cloned.1.call-done
  3243.3 31.4 all-gather.2.cloned.1.call-done
  3325.5 31.4 all-gather.2.cloned.1.call-done
  3407.8 31.4 all-gather.2.cloned.1.call-done
  3572.0 31.4 all-gather.2.cloned.1.call-done
  4064.0 31.4 all-gather.2.cloned.1.call-done
  4392.4 31.4 all-gather.2.cloned.1.call-done
  4474.7 31.4 all-gather.2.cloned.1.call-done
  4556.9 31.4 all-gather.2.cloned.1.call-done
  4885.3 31.4 all-gather.2.cloned.1.call-done
  4967.6 31.4 all-gather.2.cloned.1.call-done
  (807 shorter events, 4478.0 us)
Async XLA Ops:
  118.9 35.7 all-gather.2.cloned.1.call-start
  529.3 35.7 all-gather.2.cloned.1.call-start
  611.6 35.7 all-gather.2.cloned.1.call-start
  693.8 35.7 all-gather.2.cloned.1.call-start
  1022.2 35.7 all-gather.2.cloned.1.call-start
  1514.2 35.7 all-gather.2.cloned.1.call-start
  1760.7 35.7 all-gather.2.cloned.1.call-start
  1843.0 35.7 all-gather.2.cloned.1.call-start
  2007.2 35.7 all-gather.2.cloned.1.call-start
  2253.3 35.7 all-gather.2.cloned.1.call-start
  2335.6 35.7 all-gather.2.cloned.1.call-start
  2582.1 35.7 all-gather.2.cloned.1.call-start
  2828.5 35.7 all-gather.2.cloned.1.call-start
  3074.7 35.7 all-gather.2.cloned.1.call-start
  3238.9 35.7 all-gather.2.cloned.1.call-start
  3321.2 35.7 all-gather.2.cloned.1.call-start
  3403.4 35.7 all-gather.2.cloned.1.call-start
  3567.6 35.7 all-gather.2.cloned.1.call-start
  4059.6 35.7 all-gather.2.cloned.1.call-start
  4388.0 35.7 all-gather.2.cloned.1.call-start
  4470.3 35.7 all-gather.2.cloned.1.call-start
  4552.6 35.7 all-gather.2.cloned.1.call-start
  4881.0 35.7 all-gather.2.cloned.1.call-start
  4963.2 35.7 all-gather.2.cloned.1.call-start
  (104 other events, 4300.7 us)
Sparse Core Ops, SparseCore 0:
  122.2 32.4 all-gather.1
  286.4 32.4 all-gather.1
  368.3 32.4 all-gather.1
  450.3 32.4 all-gather.1
  614.8 32.4 all-gather.1
  697.1 32.4 all-gather.1
  943.2 32.4 all-gather.1
  1107.4 32.4 all-gather.1
  1353.3 32.4 all-gather.1
  2010.4 32.4 all-gather.1
  2338.8 32.4 all-gather.1
  2585.3 32.4 all-gather.1
  2831.7 32.4 all-gather.1
  2913.7 32.4 all-gather.1
  3077.9 32.4 all-gather.1
  3159.9 32.4 all-gather.1
  3324.4 32.4 all-gather.1
  3406.6 32.4 all-gather.1
  3816.7 32.4 all-gather.1
  4062.9 32.4 all-gather.1
  4144.8 32.4 all-gather.1
  4309.0 32.4 all-gather.1
  4720.0 32.4 all-gather.1
  4884.2 32.4 all-gather.1
  (39 shorter events, 1262.6 us)
where the time goes:
time: 5230 us; the launch traced here: 5220 us
  waiting for transfers between devices  1970 us (38%)
  matrix products  1510 us (29%)
  blocking collectives  1430 us (27%)
  local copies, waits for them, and re-layouts  174 us (3%)
  other arithmetic  116 us (2%)
    all_gather x63, waiting for transfers between devices, one_step(): lax.all_gather(state_prob.astype(jnp.bfloat16), 'states', axis=1, tiled=T...  1970 us
    dot_general x63, matrix products, one_step(): jnp.dot(gathered, trans_cols, preferred_element_type=jnp.float32)  1510 us
    psum x63, blocking collectives, one_step(): step_norm = lax.psum(jnp.sum(new_prob, axis=1), 'states')  1400 us
    gather x64, local copies, waits for them, and re-layouts, emission(): return jnp.take(emit_rows, token_col, axis=1).T.astype(jnp.float32)  173 us
  transfers between devices with their start and end apart: 63, of which 63 were waited for; matrix products, arithmetic and copies ran while one was open for 4% of the time, Pallas kernels for 0%

commit v1 on v0

v1 whole, which is shorter than its diff:
```python
import functools

import jax
import jax.numpy as jnp
from jax import lax
from jax.experimental import pallas as pl
from jax.experimental.pallas import tpu as pltpu
from jax.sharding import PartitionSpec as P

N_DEV = 8
SEQS = 128
OWN = 2048
PIECE = 512
WIDE = 256
STEPS = 63
BF16 = jnp.bfloat16
F32 = jnp.float32


def place(g, k):
    late = g // 6
    mid = (g + 6) // 8 - late
    r = g % 2 + mid * (2 + 2 * (k % 2)) + late * 6
    j = mid * (k // 2 + 2 * (g // 4)) + (1 - mid) * k
    return r, j


def step_kernel(m, steps, depth, t0_ref, a_hbm, e_hbm, st_in, len_row, len_col, ll_in, st_out, ll_out,
                fixed, ring, gath, e_buf, st, acc, part, sums, recip,
                fixed_sem, ring_sem, e_sem, st_sem, recv_sem, own_sem, fwd_sem, c_send, c_recv):
    me = lax.axis_index("states")
    core = me % 2
    xx = (me // 2) % 2
    yy = me // 4

    def dev(r):
        return me + (r % 2) * (1 - 2 * core) + ((r // 2) % 2) * (2 - 4 * xx) + (r // 4) * (4 - 8 * yy)

    def remote(src, dst, send, recv, r):
        return pltpu.make_async_remote_copy(
            src_ref=src, dst_ref=dst, send_sem=send, recv_sem=recv,
            device_id={"states": dev(r)}, device_id_type=pl.DeviceIdType.MESH,
        )

    def rows_of(g, k):
        r, j = place(g, k)
        return a_hbm.at[pl.ds(pl.multiple_of(dev(r) * OWN + j * PIECE, PIECE), PIECE)]

    def ring_copy(g):
        return pltpu.make_async_copy(rows_of(g, 3), ring.at[g % depth], ring_sem.at[g % depth])

    def start_fixed(g):
        for k in range(3):
            pltpu.make_async_copy(rows_of(g, k), fixed.at[3 * g + k], fixed_sem.at[g]).start()

    def wait_fixed(g):
        pltpu.make_async_copy(fixed.at[pl.ds(3 * g, 3)], fixed.at[pl.ds(3 * g, 3)], fixed_sem.at[g]).wait()

    def send_piece(slot, j):
        src = gath.at[slot, j]
        x_pos = 8 + 8 * (j // 2) + 2 * (j % 2)
        for r, pos in ((2, x_pos), (4, x_pos + 1), (1, 4 + j)):
            remote(src, gath.at[slot, pos], own_sem.at[slot], recv_sem.at[slot, pos], r).start()

    def received(slot, pos):
        pltpu.make_async_copy(gath.at[slot, pos], gath.at[slot, pos], recv_sem.at[slot, pos]).wait()

    def forward(slot, pos, to, r):
        remote(gath.at[slot, pos], gath.at[slot, to], fwd_sem.at[slot], recv_sem.at[slot, to], r).start()

    def product(slot, g, n):
        cols = slice(n * WIDE, (n + 1) * WIDE)
        got = jnp.dot(gath[slot, 4 * g], fixed[3 * g, :, cols], preferred_element_type=F32)
        for k in range(1, 4):
            rows = fixed[3 * g + k, :, cols] if k < 3 else ring[g % depth, :, cols]
            got = got + jnp.dot(gath[slot, 4 * g + k], rows, preferred_element_type=F32)
        return got

    def begin_group(s, g):
        ring_copy((g + depth - 1) % 8).start()

        @pl.when(s == 0)
        def _():
            wait_fixed(g)

            @pl.when(g + 2 < 8)
            def _():
                start_fixed(g + 2)

        ring_copy(g).wait()

    st_copy = pltpu.make_async_copy(st_in.at[pl.ds(0, m)], st, st_sem.at[0])
    st_copy.start()
    ring_copy(0).start()
    start_fixed(0)
    for g in range(1, depth - 1):
        ring_copy(g).start()
    start_fixed(1)
    pltpu.make_async_copy(e_hbm.at[0], e_buf, e_sem.at[0]).start()

    barrier = pltpu.get_barrier_semaphore()
    for r in range(1, N_DEV):
        pl.semaphore_signal(barrier, inc=1, device_id={"states": dev(r)}, device_id_type=pl.DeviceIdType.MESH)

    ll_out[...] = ll_in[...]
    if m < SEQS:
        sums[...] = jnp.zeros_like(sums)
    t0 = t0_ref[0]
    lens_row = len_row[...]

    st_copy.wait()
    pl.semaphore_wait(barrier, N_DEV - 1)
    for j in range(4):
        gath[0, j] = st[:, j * PIECE:(j + 1) * PIECE].astype(BF16)
        if j:
            send_piece(0, j - 1)
    send_piece(0, 3)

    def one_step(s, carry):
        slot = s % 2
        then = 1 - slot

        begin_group(s, 0)
        for n in range(8):
            acc[n] = product(slot, 0, n)

        def group(g, carry):
            for k in range(4):
                pos = 4 * g + k
                received(slot, pos)
                if k % 2 == 0:
                    @pl.when(g == 2)
                    def _():
                        forward(slot, pos, 24 + k // 2, 4)
                else:
                    @pl.when(g == 4)
                    def _():
                        forward(slot, pos, 26 + k // 2, 2)

                @pl.when(g % 2 == 0)
                def _():
                    forward(slot, pos, pos + 4, 1)

            begin_group(s, g)
            for n in range(8):
                acc[n] += product(slot, g, n)
            return carry

        lax.fori_loop(1, 7, group, 0)

        for k in range(4):
            received(slot, 28 + k)
        begin_group(s, 7)
        pltpu.make_async_copy(e_hbm.at[s], e_buf, e_sem.at[0]).wait()
        both = jnp.zeros((m, 128), F32)
        for n in range(8):
            a = (acc[n] + product(slot, 7, n)) * e_buf[:, n * WIDE:(n + 1) * WIDE].astype(F32)
            acc[n] = a
            both = both + (a[:, :128] + a[:, 128:])
        sums[:m] = both

        part[slot, me] = jnp.sum(sums[...].T.reshape(16, 8, 128), axis=0)
        for r in range(1, N_DEV):
            remote(part.at[slot, me], part.at[slot, me], c_send.at[slot], c_recv.at[slot], r).start()

        @pl.when(s + 1 < steps)
        def _():
            pltpu.make_async_copy(e_hbm.at[s + 1], e_buf, e_sem.at[0]).start()

        pltpu.make_async_copy(gath.at[slot, pl.ds(0, 12)], gath.at[slot, pl.ds(0, 12)], own_sem.at[slot]).wait()
        pltpu.make_async_copy(gath.at[slot, pl.ds(0, 16)], gath.at[slot, pl.ds(0, 16)], fwd_sem.at[slot]).wait()
        pltpu.make_async_copy(part.at[slot, pl.ds(0, 7)], part.at[slot, pl.ds(0, 7)], c_recv.at[slot]).wait()
        whole = part[slot, 0]
        for d in range(1, N_DEV):
            whole = whole + part[slot, d]
        norm = jnp.sum(whole, axis=0, keepdims=True)
        recip[...] = jnp.broadcast_to(1.0 / norm, (128, 128)).T
        t = t0 + s
        ll_out[...] = ll_out[...] + jnp.where(t < lens_row, jnp.log(norm), 0.0)
        pltpu.make_async_copy(part.at[slot, pl.ds(0, 7)], part.at[slot, pl.ds(0, 7)], c_send.at[slot]).wait()

        scale = recip[:m]
        live = t < len_col[:m]
        for j in range(4):
            for q in range(4):
                at = j * PIECE + q * 128
                cols = slice(at, at + 128)
                new = jnp.where(live, acc[at // WIDE, :, (q % 2) * 128:(q % 2 + 1) * 128] * scale, st[:, cols])
                st[:, cols] = new
                gath[then, j, :, q * 128:(q + 1) * 128] = new.astype(BF16)
            if j:
                @pl.when(s + 1 < steps)
                def _():
                    send_piece(then, j - 1)

        @pl.when(s + 1 < steps)
        def _():
            send_piece(then, 3)

        return carry

    lax.fori_loop(0, steps, one_step, 0)

    for g in range(depth - 1):
        ring_copy(g).wait()
    out_copy = pltpu.make_async_copy(st, st_out.at[pl.ds(0, m)], st_sem.at[0])
    out_copy.start()
    out_copy.wait()


def run_steps(m, steps, t0, trans, emis, state, len_row, len_col, log_lik):
    vmem = pl.BlockSpec(memory_space=pltpu.VMEM)
    hbm = pl.BlockSpec(memory_space=pl.ANY)
    depth = 2 if m > 80 else 4
    dma = pltpu.SemaphoreType.DMA
    return pl.pallas_call(
        functools.partial(step_kernel, m, steps, depth),
        out_shape=(jax.ShapeDtypeStruct((SEQS, OWN), F32), jax.ShapeDtypeStruct((1, SEQS), F32)),
        in_specs=[pl.BlockSpec(memory_space=pltpu.SMEM), hbm, hbm, hbm, vmem, vmem, vmem],
        out_specs=(hbm, vmem),
        scratch_shapes=[
            pltpu.VMEM((24, PIECE, OWN), BF16),
            pltpu.VMEM((depth, PIECE, OWN), BF16),
            pltpu.VMEM((2, 32, m, PIECE), BF16),
            pltpu.VMEM((m, OWN), BF16),
            pltpu.VMEM((m, OWN), F32),
            pltpu.VMEM((8, m, WIDE), F32),
            pltpu.VMEM((2, N_DEV, 8, 128), F32),
            pltpu.VMEM((128, 128), F32),
            pltpu.VMEM((128, 128), F32),
            dma((8,)), dma((depth,)), dma((1,)), dma((1,)), dma((2, 32)), dma((2,)), dma((2,)), dma((2,)), dma((2,)),
        ],
        input_output_aliases={3: 0},
        compiler_params=pltpu.CompilerParams(
            collective_id=0, has_side_effects=True, vmem_limit_bytes=67043328
        ),
        name=f"steps_{m}",
    )(t0, trans, emis, state, len_row, len_col, log_lik)


def solution(mesh):
    def local_run(trans_cols, emit_rows, init_part, token_rows, length_rows):
        emit_t = emit_rows.T
        first_prob = init_part[None, :] * jnp.take(emit_t, token_rows[:, 0], axis=0, mode="clip").astype(F32)
        first_norm = lax.psum(jnp.sum(first_prob, axis=1), "states")
        state = first_prob / first_norm[:, None]
        log_lik = jnp.log(first_norm)[None, :]
        tokens = token_rows[:, 1:].T.reshape(-1)
        emis = jnp.take(emit_t, tokens, axis=0, mode="clip").reshape(STEPS, SEQS, OWN)
        len_row = length_rows[None, :]
        len_col = jnp.broadcast_to(length_rows[:, None], (SEQS, 128))
        t0 = jnp.ones((1,), jnp.int32)
        state, log_lik = run_steps(SEQS, STEPS, t0, trans_cols, emis, state, len_row, len_col, log_lik)
        return log_lik[0], state

    return jax.shard_map(
        local_run,
        mesh=mesh,
        in_specs=(P(None, "states"), P("states", None), P("states"), P("seqs", None), P("seqs")),
        out_specs=(P("seqs"), P("seqs", "states")),
        check_vma=False,
    )
```

time: 5230 us -> 1720 us (0.33)
  waiting for transfers between devices: 1970 us -> 0 us
  Pallas kernels: 0 us -> 1590 us
  matrix products: 1510 us -> 0 us
  blocking collectives: 1430 us -> 25.1 us
  other arithmetic: 116 us -> 2.76 us
  local copies, waits for them, and re-layouts: 174 us -> 94.8 us
    all_gather x63 -> x0, waiting for transfers between devices: 1970 us -> none  [one_step(): lax.all_gather(state_prob.astype(jnp.bfloat16), 'states', axis=1, tiled=T...]
    pallas_call x0 -> x1, Pallas kernels: none -> 1590 us  [run_steps(): pl.pallas_call(functools.partial(step_kernel, m, steps, depth), out_shape...]
    dot_general x63 -> x0, matrix products: 1510 us -> none  [one_step(): jnp.dot(gathered, trans_cols, preferred_element_type=jnp.float32)]
    psum x63 -> x0, blocking collectives: 1400 us -> none  [one_step(): step_norm = lax.psum(jnp.sum(new_prob, axis=1), 'states')]
    gather x64 -> x2, local copies, waits for them, and re-layouts: 173 us -> 88 us  [the longest x1 85.3 us: local_run(): jnp.take(emit_t, tokens, axis=0, mode='clip').reshape(STEPS, SEQS, OWN)]
    convert_element_type x63 -> x0, other arithmetic: 54 us -> none  [one_step(): state_prob.astype(jnp.bfloat16)]
  transfers between devices with their start and end apart: 63 -> 0, of which waited for: 63 -> 0; matrix products, arithmetic and copies ran while one was open for 4% -> 0% of each run, Pallas kernels for 0% -> 0%
where the time goes in v1:
time: 1720 us
  Pallas kernels  1590 us (92%)
  local copies, waits for them, and re-layouts  94.8 us (6%)
  blocking collectives  25.1 us (1%)
    pallas_call x1, Pallas kernels, run_steps(): pl.pallas_call(functools.partial(step_kernel, m, steps, depth), out_shape...  1590 us
    gather x1, local copies, waits for them, and re-layouts, local_run(): jnp.take(emit_t, tokens, axis=0, mode='clip').reshape(STEPS, SEQS, OWN)  85.3 us

profile of v1, /device:TPU:0, one launch (start us, length us, event | category | flops | bytes accessed | tf_op | source)
XLA Modules:
  0.0 1716.0 jit_solution(5989661513740027171)
XLA Ops:
  0.6 0.7 slice_bitcast_fusion.1
  1.3 0.8 slice_bitcast_fusion
  2.1 1.4 broadcast_in_dim.22.len_col
  3.5 2.7 gather_fusion.1
  6.2 0.9 fusion.1
  7.1 25.1 %psum.7 = f32[128]{0:T(128)S(1)} all-reduce(f32[128]{0:T(128)S(1)} %fusion.1), channel_id=1, replica_groups=mesh['seqs'=1,'states'=8] {'states'}, use_global_device_ids=true, to_apply=%region_1.2 | all-reduce | flops 128 | bytes 1024 | tf_op jit(solution)/shard_map/psum | solution.py:245
  32.1 0.5 log_bitcast_fusion.ll_in
  32.7 1.9 fusion.st_in
  34.5 85.3 %gather_fusion = bf16[8064,2048]{1,0:T(8,128)(2,1)} fusion(bf16[10000,2048]{1,0:T(8,128)(2,1)} %bitcast.13, s32[8192]{0:T(1024)S(1)} %pad_clamp_fusion), kind=kCustom, calls=%fused_computation | custom fusion | bytes 66092544 | tf_op jit(solution)/shard_map/jit(_take)/gather | solution.py:249
  119.8 1592.8 %steps_128.1 = (f32[128,2048]{1,0:T(8,128)}, f32[1,128]{1,0:T(1,128)}) custom-call(s32[1]{0:T(128)} %constant.0.clone.1.t0_ref, bf16[16384,2048]{1,0:T(8,128)(2,1)} %a_hbm.1, bf16[63,128,2048]{2,1,0:T(8,128)(2,1)} %bitcast.14, f32[128,2048]{1,0:T(8,128)} %fusion.st_in, s32[1,128]{1,0:T(1,128)} %bitcast.15, ...), custom_call_target="tpu_custom_call", output_to_operand_aliasing={{0}: (3, {})} | custom-call | tf_op jit(solution)/shard_map/steps_128/pallas_call | solution.py:216
  1712.5 1.2 copy.11
  1713.7 2.3 copy.12
  (2 shorter events, 0.0 us)

commit v2 on v1

--- a/solution.py
+++ b/solution.py
@@ -13,6 +13,8 @@
 PIECE = 512
 WIDE = 256
 STEPS = 63
+SEGMENT = 9
+ROWS = (48, 64, 80, 96, 112, 128)
 BF16 = jnp.bfloat16
 F32 = jnp.float32
 
@@ -25,22 +27,89 @@
     return r, j
 
 
+def distances(me):
+    core = me % 2
+    xx = (me // 2) % 2
+    yy = me // 4
+
+    def dev(r):
+        return me + (r % 2) * (1 - 2 * core) + ((r // 2) % 2) * (2 - 4 * xx) + (r // 4) * (4 - 8 * yy)
+
+    return dev
+
+
+def remote_copy(dev, src, dst, send, recv, r):
+    return pltpu.make_async_remote_copy(
+        src_ref=src, dst_ref=dst, send_sem=send, recv_sem=recv,
+        device_id={"states": dev(r)}, device_id_type=pl.DeviceIdType.MESH,
+    )
+
+
+def signal_all(dev):
+    barrier = pltpu.get_barrier_semaphore()
+    for r in range(1, N_DEV):
+        pl.semaphore_signal(barrier, inc=1, device_id={"states": dev(r)}, device_id_type=pl.DeviceIdType.MESH)
+    return barrier
+
+
+def send_sums(me, dev, sums, part, send, recv):
+    part[me] = jnp.sum(sums[...].T.reshape(16, 8, 128), axis=0)
+    for r in range(1, N_DEV):
+        remote_copy(dev, part.at[me], part.at[me], send, recv, r).start()
+
+
+def add_sums(part, recv):
+    pltpu.make_async_copy(part.at[pl.ds(0, 7)], part.at[pl.ds(0, 7)], recv).wait()
+    whole = part[0]
+    for d in range(1, N_DEV):
+        whole = whole + part[d]
+    return jnp.sum(whole, axis=0, keepdims=True)
+
+
+def first_kernel(raw, alpha, ll, part, sums, send, recv):
+    me = lax.axis_index("states")
+    dev = distances(me)
+    barrier = signal_all(dev)
+    both = jnp.zeros((SEQS, 128), F32)
+    for q in range(16):
+        both = both + raw[:, q * 128:(q + 1) * 128]
+    sums[...] = both
+    pl.semaphore_wait(barrier, N_DEV - 1)
+    send_sums(me, dev, sums, part, send, recv)
+    norm = add_sums(part, recv)
+    ll[...] = jnp.log(norm)
+    scale = jnp.broadcast_to(1.0 / norm, (128, 128)).T
+    for q in range(16):
+        alpha[:, q * 128:(q + 1) * 128] = raw[:, q * 128:(q + 1) * 128] * scale
+    pltpu.make_async_copy(part.at[pl.ds(0, 7)], part.at[pl.ds(0, 7)], send).wait()
+
+
+def run_first(number, raw):
+    vmem = pl.BlockSpec(memory_space=pltpu.VMEM)
+    return pl.pallas_call(
+        first_kernel,
+        out_shape=(jax.ShapeDtypeStruct((SEQS, OWN), F32), jax.ShapeDtypeStruct((1, SEQS), F32)),
+        in_specs=[vmem],
+        out_specs=(vmem, vmem),
+        scratch_shapes=[
+            pltpu.VMEM((N_DEV, 8, 128), F32),
+            pltpu.VMEM((128, 128), F32),
+            pltpu.SemaphoreType.DMA,
+            pltpu.SemaphoreType.DMA,
+        ],
+        compiler_params=pltpu.CompilerParams(collective_id=number, has_side_effects=True, vmem_limit_bytes=8 << 20),
+        name="first",
+    )(raw)
+
+
 def step_kernel(m, steps, depth, t0_ref, a_hbm, e_hbm, st_in, len_row, len_col, ll_in, st_out, ll_out,
                 fixed, ring, gath, e_buf, st, acc, part, sums, recip,
                 fixed_sem, ring_sem, e_sem, st_sem, recv_sem, own_sem, fwd_sem, c_send, c_recv):
     me = lax.axis_index("states")
-    core = me % 2
-    xx = (me // 2) % 2
-    yy = me // 4
-
-    def dev(r):
-        return me + (r % 2) * (1 - 2 * core) + ((r // 2) % 2) * (2 - 4 * xx) + (r // 4) * (4 - 8 * yy)
+    dev = distances(me)
 
     def remote(src, dst, send, recv, r):
-        return pltpu.make_async_remote_copy(
-            src_ref=src, dst_ref=dst, send_sem=send, recv_sem=recv,
-            device_id={"states": dev(r)}, device_id_type=pl.DeviceIdType.MESH,
-        )
+        return remote_copy(dev, src, dst, send, recv, r)
 
     def rows_of(g, k):
         r, j = place(g, k)
@@ -98,16 +167,24 @@
     start_fixed(1)
     pltpu.make_async_copy(e_hbm.at[0], e_buf, e_sem.at[0]).start()
 
-    barrier = pltpu.get_barrier_semaphore()
-    for r in range(1, N_DEV):
-        pl.semaphore_signal(barrier, inc=1, device_id={"states": dev(r)}, device_id_type=pl.DeviceIdType.MESH)
-
-    ll_out[...] = ll_in[...]
+    barrier = signal_all(dev)
     if m < SEQS:
         sums[...] = jnp.zeros_like(sums)
     t0 = t0_ref[0]
     lens_row = len_row[...]
 
+    def total(slot):
+        send_sums(me, dev, sums, part.at[slot], c_send.at[slot], c_recv.at[slot])
+
+    def total_done(slot):
+        norm = add_sums(part.at[slot], c_recv.at[slot])
+        recip[...] = jnp.broadcast_to(1.0 / norm, (128, 128)).T
+        return norm
+
+    def total_sent(slot):
+        pltpu.make_async_copy(part.at[slot, pl.ds(0, 7)], part.at[slot, pl.ds(0, 7)], c_send.at[slot]).wait()
+
+    ll_out[...] = ll_in[...]
     st_copy.wait()
     pl.semaphore_wait(barrier, N_DEV - 1)
     for j in range(4):
@@ -120,14 +197,14 @@
         slot = s % 2
         then = 1 - slot
 
-        begin_group(s, 0)
-        for n in range(8):
-            acc[n] = product(slot, 0, n)
-
         def group(g, carry):
             for k in range(4):
                 pos = 4 * g + k
-                received(slot, pos)
+
+                @pl.when(g >= 1)
+                def _():
+                    received(slot, pos)
+
                 if k % 2 == 0:
                     @pl.when(g == 2)
                     def _():
@@ -137,16 +214,16 @@
                     def _():
                         forward(slot, pos, 26 + k // 2, 2)
 
-                @pl.when(g % 2 == 0)
+                @pl.when((1 - g % 2) * g > 0)
                 def _():
                     forward(slot, pos, pos + 4, 1)
 
             begin_group(s, g)
             for n in range(8):
-                acc[n] += product(slot, g, n)
+                acc[n] = jnp.where(g > 0, acc[n], 0.0) + product(slot, g, n)
             return carry
 
-        lax.fori_loop(1, 7, group, 0)
+        lax.fori_loop(0, 7, group, 0)
 
         for k in range(4):
             received(slot, 28 + k)
@@ -159,9 +236,7 @@
             both = both + (a[:, :128] + a[:, 128:])
         sums[:m] = both
 
-        part[slot, me] = jnp.sum(sums[...].T.reshape(16, 8, 128), axis=0)
-        for r in range(1, N_DEV):
-            remote(part.at[slot, me], part.at[slot, me], c_send.at[slot], c_recv.at[slot], r).start()
+        total(slot)
 
         @pl.when(s + 1 < steps)
         def _():
@@ -169,15 +244,10 @@
 
         pltpu.make_async_copy(gath.at[slot, pl.ds(0, 12)], gath.at[slot, pl.ds(0, 12)], own_sem.at[slot]).wait()
         pltpu.make_async_copy(gath.at[slot, pl.ds(0, 16)], gath.at[slot, pl.ds(0, 16)], fwd_sem.at[slot]).wait()
-        pltpu.make_async_copy(part.at[slot, pl.ds(0, 7)], part.at[slot, pl.ds(0, 7)], c_recv.at[slot]).wait()
-        whole = part[slot, 0]
-        for d in range(1, N_DEV):
-            whole = whole + part[slot, d]
-        norm = jnp.sum(whole, axis=0, keepdims=True)
-        recip[...] = jnp.broadcast_to(1.0 / norm, (128, 128)).T
+        norm = total_done(slot)
         t = t0 + s
         ll_out[...] = ll_out[...] + jnp.where(t < lens_row, jnp.log(norm), 0.0)
-        pltpu.make_async_copy(part.at[slot, pl.ds(0, 7)], part.at[slot, pl.ds(0, 7)], c_send.at[slot]).wait()
+        total_sent(slot)
 
         scale = recip[:m]
         live = t < len_col[:m]
@@ -208,7 +278,7 @@
     out_copy.wait()
 
 
-def run_steps(m, steps, t0, trans, emis, state, len_row, len_col, log_lik):
+def run_steps(m, steps, number, t0, trans, emis, state, len_row, len_col, log_lik):
     vmem = pl.BlockSpec(memory_space=pltpu.VMEM)
     hbm = pl.BlockSpec(memory_space=pl.ANY)
     depth = 2 if m > 80 else 4
@@ -232,26 +302,43 @@
         ],
         input_output_aliases={3: 0},
         compiler_params=pltpu.CompilerParams(
-            collective_id=0, has_side_effects=True, vmem_limit_bytes=67043328
+            collective_id=number, has_side_effects=True, vmem_limit_bytes=67043328
         ),
-        name=f"steps_{m}",
+        name=f"steps_{m}_{number}",
     )(t0, trans, emis, state, len_row, len_col, log_lik)
 
 
 def solution(mesh):
     def local_run(trans_cols, emit_rows, init_part, token_rows, length_rows):
         emit_t = emit_rows.T
-        first_prob = init_part[None, :] * jnp.take(emit_t, token_rows[:, 0], axis=0, mode="clip").astype(F32)
-        first_norm = lax.psum(jnp.sum(first_prob, axis=1), "states")
-        state = first_prob / first_norm[:, None]
-        log_lik = jnp.log(first_norm)[None, :]
-        tokens = token_rows[:, 1:].T.reshape(-1)
-        emis = jnp.take(emit_t, tokens, axis=0, mode="clip").reshape(STEPS, SEQS, OWN)
-        len_row = length_rows[None, :]
-        len_col = jnp.broadcast_to(length_rows[:, None], (SEQS, 128))
-        t0 = jnp.ones((1,), jnp.int32)
-        state, log_lik = run_steps(SEQS, STEPS, t0, trans_cols, emis, state, len_row, len_col, log_lik)
-        return log_lik[0], state
+
+        def emissions(tokens):
+            return jnp.take(emit_t, tokens.reshape(-1), axis=0, mode="clip").reshape(*tokens.shape, OWN)
+
+        key = length_rows * SEQS + (SEQS - 1 - jnp.arange(SEQS, dtype=jnp.int32))
+        rank = jnp.sum((key[None, :] > key[:, None]).astype(jnp.int32), axis=1)
+        pick = (rank[None, :] == jnp.arange(SEQS, dtype=jnp.int32)[:, None]).astype(jnp.int32)
+        lens = jnp.sum(pick * length_rows[None, :], axis=1)
+        tokens = jnp.sum(token_rows.T[:, None, :] * pick[None], axis=2)
+        len_row = lens[None, :]
+        len_col = jnp.broadcast_to(lens[:, None], (SEQS, 128))
+
+        def segment(m, number, t0, state, log_lik):
+            part = lax.dynamic_slice_in_dim(tokens, t0, SEGMENT, axis=0)[:, :m]
+            return run_steps(m, SEGMENT, number, jnp.reshape(t0, (1,)), trans_cols, emissions(part), state,
+                             len_row, len_col, log_lik)
+
+        state, log_lik = run_first(0, init_part[None, :] * emissions(tokens[0]).astype(F32))
+
+        def later(seg, carried):
+            t0 = 1 + SEGMENT * seg
+            live = jnp.sum((lens > t0).astype(jnp.int32))
+            which = sum((live > m).astype(jnp.int32) for m in ROWS[:-1])
+            branches = [functools.partial(segment, m, 1 + i) for i, m in enumerate(ROWS)]
+            return lax.switch(which, branches, t0, *carried)
+
+        state, log_lik = lax.fori_loop(0, STEPS // SEGMENT, later, (state, log_lik))
+        return jnp.take(log_lik[0], rank, mode="clip"), jnp.take(state, rank, axis=0, mode="clip")
 
     return jax.shard_map(
         local_run,

time: 1720 us -> 1570 us (0.913)
  Pallas kernels: 1590 us -> 1400 us
  local copies, waits for them, and re-layouts: 94.8 us -> 130 us
  blocking collectives: 25.1 us -> 0 us
  loops' own time: 0 us -> 22.9 us
    pallas_call x1 -> x7, Pallas kernels: 1590 us -> 1390 us  [run_steps(): pl.pallas_call(functools.partial(step_kernel, m, steps, depth), out_shape...]
    psum x1 -> x0, blocking collectives: 25.1 us -> none  [local_run(): first_norm = lax.psum(jnp.sum(first_prob, axis=1), 'states')]
    another operation x0 -> x8, loops' own time: none -> 22.9 us  [the longest x1 22.8 us: local_run(): state, log_lik = lax.fori_loop(0, STEPS // SEGMENT, later, (state, log_lik))]
    gather x2 -> x10, local copies, waits for them, and re-layouts: 88 us -> 107 us  [the longest x8 102 us: emissions(): jnp.take(emit_t, tokens.reshape(-1), axis=0, mode='clip')]
where the time goes in v2:
time: 1570 us; the launch traced here: 1560 us
  Pallas kernels  1400 us (89%)
  local copies, waits for them, and re-layouts  130 us (8%)
  loops' own time  22.9 us (1%)
    pallas_call x7, Pallas kernels, run_steps(): pl.pallas_call(functools.partial(step_kernel, m, steps, depth), out_shape...  1390 us
    gather x8, local copies, waits for them, and re-layouts, emissions(): jnp.take(emit_t, tokens.reshape(-1), axis=0, mode='clip')  102 us

profile of v2, /device:TPU:0, one launch (start us, length us, event | category | flops | bytes accessed | tf_op | source)
XLA Modules:
  0.0 1565.0 jit_solution(13574274068126148576)
XLA Ops:
  7.6 7.8 first.1
  16.1 1542.9 %while.17 = (s32[]{:T(128)}, f32[128,2048]{1,0:T(8,128)}, f32[1,128]{1,0:T(1,128)}, s32[128]{0:T(128)}, s32[64,128]{1,0:T(8,128)}, /*index=5*/bf16[10000,2048]{1...) while((s32[]{:T(128)}, f32[128,2048]{1,0:T(8,128)}, ...), condition=%wide.region_11.12_spmd.clone.clone, body=%wide.region_3.11_spmd.clone.clone.sunk | while | flops 2453 | bytes 9531825 | solution.py:340
  21.8 252.8 %conditional.4 = ((f32[128,2048]{1,0:T(8,128)}, f32[1,128]{1,0:T(1,128)})) conditional(s32[]{:T(128)} %clamp.27, (s32[]{:T(128)}, s32[64,128]{1,0:T(8,128)}, bf16[10000,2048]{1,0:T(8,128)(2,1)}, bf16[16384,2048]{1,0:T(8,128)(2,1)}, f32[128,2048]{1,0:T(8,128)}, /*index=5*/s32[1,128]{1,0:T(1,128)}, ...), branch_computations={%region_5.5_spmd, %region_6.6_spmd, %region_7.7_spmd, %region_8.8_... | conditional | flops 2051 | bytes 9463854 | solution.py:338
  22.6 17.4 %gather_fusion.5 = bf16[1152,2048]{1,0:T(8,128)(2,1)} fusion(bf16[10000,2048]{1,0:T(8,128)(2,1)} %get-tuple-element.285, s32[2048]{0:T(1024)S(1)} %pad_clamp_fusion.5), kind=kCustom, calls=%fused_computation.5 | custom fusion | bytes 9441792 | tf_op jit(solution)/shard_map/while/body/eval_jaxpr/cond/branch_5_fun/jit(_take)/gather | solution.py:316
  40.0 234.6 %steps_128_6.1 = (f32[128,2048]{1,0:T(8,128)}, f32[1,128]{1,0:T(1,128)}) custom-call(s32[1]{0:T(128)} %bitcast.10.t0_ref, bf16[16384,2048]{1,0:T(8,128)(2,1)} %get-tuple-element.284.a_hbm, bf16[9,128,2048]{2,1,0:T(8,128)(2,1)} %bitcast.23, f32[128,2048]{1,0:T(8,128)} %get-tuple-element.287.st_in, ...), custom_call_target="tpu_custom_call", output_to_operand_aliasing={{0}: (3, {})} | custom-call | tf_op jit(solution)/shard_map/while/body/eval_jaxpr/cond/branch_5_fun/steps_128_6/pallas_call | solution.py:286
  281.6 244.9 %conditional.4 = ((f32[128,2048]{1,0:T(8,128)}, f32[1,128]{1,0:T(1,128)})) conditional(s32[]{:T(128)} %clamp.27, (s32[]{:T(128)}, s32[64,128]{1,0:T(8,128)}, bf16[10000,2048]{1,0:T(8,128)(2,1)}, bf16[16384,2048]{1,0:T(8,128)(2,1)}, f32[128,2048]{1,0:T(8,128)}, /*index=5*/s32[1,128]{1,0:T(1,128)}, ...), branch_computations={%region_5.5_spmd, %region_6.6_spmd, %region_7.7_spmd, %region_8.8_... | conditional | flops 2051 | bytes 9463854 | solution.py:338
  282.4 24.6 %gather_fusion.4 = bf16[1008,2048]{1,0:T(8,128)(2,1)} fusion(bf16[10000,2048]{1,0:T(8,128)(2,1)} %get-tuple-element.277, s32[1024]{0:T(1024)S(1)} %pad_clamp_fusion.4), kind=kCustom, calls=%fused_computation.4 | custom fusion | bytes 8261568 | tf_op jit(solution)/shard_map/while/body/eval_jaxpr/cond/branch_4_fun/jit(_take)/gather | solution.py:316
  307.0 219.5 %steps_112_5.1 = (f32[128,2048]{1,0:T(8,128)}, f32[1,128]{1,0:T(1,128)}) custom-call(s32[1]{0:T(128)} %bitcast.8.t0_ref, bf16[16384,2048]{1,0:T(8,128)(2,1)} %get-tuple-element.276.a_hbm, bf16[9,112,2048]{2,1,0:T(8,128)(2,1)} %bitcast.24, f32[128,2048]{1,0:T(8,128)} %get-tuple-element.279.st_in, ...), custom_call_target="tpu_custom_call", output_to_operand_aliasing={{0}: (3, {})} | custom-call | tf_op jit(solution)/shard_map/while/body/eval_jaxpr/cond/branch_4_fun/steps_112_5/pallas_call | solution.py:286
  533.5 224.7 %conditional.4 = ((f32[128,2048]{1,0:T(8,128)}, f32[1,128]{1,0:T(1,128)})) conditional(s32[]{:T(128)} %clamp.27, (s32[]{:T(128)}, s32[64,128]{1,0:T(8,128)}, bf16[10000,2048]{1,0:T(8,128)(2,1)}, bf16[16384,2048]{1,0:T(8,128)(2,1)}, f32[128,2048]{1,0:T(8,128)}, /*index=5*/s32[1,128]{1,0:T(1,128)}, ...), branch_computations={%region_5.5_spmd, %region_6.6_spmd, %region_7.7_spmd, %region_8.8_... | conditional | flops 2051 | bytes 9463854 | solution.py:338
  534.3 15.8 %gather_fusion.3 = bf16[864,2048]{1,0:T(8,128)(2,1)} fusion(bf16[10000,2048]{1,0:T(8,128)(2,1)} %get-tuple-element.269, s32[1024]{0:T(1024)S(1)} %pad_clamp_fusion.3), kind=kCustom, calls=%fused_computation.3 | custom fusion | bytes 7081344 | tf_op jit(solution)/shard_map/while/body/eval_jaxpr/cond/branch_3_fun/jit(_take)/gather | solution.py:316
  550.1 208.1 %steps_96_4.1 = (f32[128,2048]{1,0:T(8,128)}, f32[1,128]{1,0:T(1,128)}) custom-call(s32[1]{0:T(128)} %bitcast.6.t0_ref, bf16[16384,2048]{1,0:T(8,128)(2,1)} %get-tuple-element.268.a_hbm, bf16[9,96,2048]{2,1,0:T(8,128)(2,1)} %bitcast.25, f32[128,2048]{1,0:T(8,128)} %get-tuple-element.271.st_in, ...), custom_call_target="tpu_custom_call", output_to_operand_aliasing={{0}: (3, {})} | custom-call | tf_op jit(solution)/shard_map/while/body/eval_jaxpr/cond/branch_3_fun/steps_96_4/pallas_call | solution.py:286
  765.2 207.8 %conditional.4 = ((f32[128,2048]{1,0:T(8,128)}, f32[1,128]{1,0:T(1,128)})) conditional(s32[]{:T(128)} %clamp.27, (s32[]{:T(128)}, s32[64,128]{1,0:T(8,128)}, bf16[10000,2048]{1,0:T(8,128)(2,1)}, bf16[16384,2048]{1,0:T(8,128)(2,1)}, f32[128,2048]{1,0:T(8,128)}, /*index=5*/s32[1,128]{1,0:T(1,128)}, ...), branch_computations={%region_5.5_spmd, %region_6.6_spmd, %region_7.7_spmd, %region_8.8_... | conditional | flops 2051 | bytes 9463854 | solution.py:338
  766.0 9.9 gather_fusion.2
  775.9 197.1 %steps_80_3.1 = (f32[128,2048]{1,0:T(8,128)}, f32[1,128]{1,0:T(1,128)}) custom-call(s32[1]{0:T(128)} %bitcast.4.t0_ref, bf16[16384,2048]{1,0:T(8,128)(2,1)} %get-tuple-element.260.a_hbm, bf16[9,80,2048]{2,1,0:T(8,128)(2,1)} %bitcast.26, f32[128,2048]{1,0:T(8,128)} %get-tuple-element.263.st_in, ...), custom_call_target="tpu_custom_call", output_to_operand_aliasing={{0}: (3, {})} | custom-call | tf_op jit(solution)/shard_map/while/body/eval_jaxpr/cond/branch_2_fun/steps_80_3/pallas_call | solution.py:286
  979.9 200.2 %conditional.4 = ((f32[128,2048]{1,0:T(8,128)}, f32[1,128]{1,0:T(1,128)})) conditional(s32[]{:T(128)} %clamp.27, (s32[]{:T(128)}, s32[64,128]{1,0:T(8,128)}, bf16[10000,2048]{1,0:T(8,128)(2,1)}, bf16[16384,2048]{1,0:T(8,128)(2,1)}, f32[128,2048]{1,0:T(8,128)}, /*index=5*/s32[1,128]{1,0:T(1,128)}, ...), branch_computations={%region_5.5_spmd, %region_6.6_spmd, %region_7.7_spmd, %region_8.8_... | conditional | flops 2051 | bytes 9463854 | solution.py:338
  980.7 14.4 gather_fusion.1
  995.2 185.0 %steps_64_2.1 = (f32[128,2048]{1,0:T(8,128)}, f32[1,128]{1,0:T(1,128)}) custom-call(s32[1]{0:T(128)} %bitcast.2.t0_ref, bf16[16384,2048]{1,0:T(8,128)(2,1)} %get-tuple-element.252.a_hbm, bf16[9,64,2048]{2,1,0:T(8,128)(2,1)} %bitcast.27, f32[128,2048]{1,0:T(8,128)} %get-tuple-element.255.st_in, ...), custom_call_target="tpu_custom_call", output_to_operand_aliasing={{0}: (3, {})} | custom-call | tf_op jit(solution)/shard_map/while/body/eval_jaxpr/cond/branch_1_fun/steps_64_2/pallas_call | solution.py:286
  1187.2 181.9 %conditional.4 = ((f32[128,2048]{1,0:T(8,128)}, f32[1,128]{1,0:T(1,128)})) conditional(s32[]{:T(128)} %clamp.27, (s32[]{:T(128)}, s32[64,128]{1,0:T(8,128)}, bf16[10000,2048]{1,0:T(8,128)(2,1)}, bf16[16384,2048]{1,0:T(8,128)(2,1)}, f32[128,2048]{1,0:T(8,128)}, /*index=5*/s32[1,128]{1,0:T(1,128)}, ...), branch_computations={%region_5.5_spmd, %region_6.6_spmd, %region_7.7_spmd, %region_8.8_... | conditional | flops 2051 | bytes 9463854 | solution.py:338
  1188.0 8.3 gather_fusion
  1196.3 172.7 %steps_48_1.1 = (f32[128,2048]{1,0:T(8,128)}, f32[1,128]{1,0:T(1,128)}) custom-call(s32[1]{0:T(128)} %bitcast.t0_ref, bf16[16384,2048]{1,0:T(8,128)(2,1)} %get-tuple-element.244.a_hbm, bf16[9,48,2048]{2,1,0:T(8,128)(2,1)} %bitcast.28, f32[128,2048]{1,0:T(8,128)} %get-tuple-element.247.st_in, ...), custom_call_target="tpu_custom_call", output_to_operand_aliasing={{0}: (3, {})} | custom-call | tf_op jit(solution)/shard_map/while/body/eval_jaxpr/cond/branch_0_fun/steps_48_1/pallas_call | solution.py:286
  1376.0 181.8 %conditional.4 = ((f32[128,2048]{1,0:T(8,128)}, f32[1,128]{1,0:T(1,128)})) conditional(s32[]{:T(128)} %clamp.27, (s32[]{:T(128)}, s32[64,128]{1,0:T(8,128)}, bf16[10000,2048]{1,0:T(8,128)(2,1)}, bf16[16384,2048]{1,0:T(8,128)(2,1)}, f32[128,2048]{1,0:T(8,128)}, /*index=5*/s32[1,128]{1,0:T(1,128)}, ...), branch_computations={%region_5.5_spmd, %region_6.6_spmd, %region_7.7_spmd, %region_8.8_... | conditional | flops 2051 | bytes 9463854 | solution.py:338
  1376.8 8.3 gather_fusion
  1385.1 172.7 %steps_48_1.1 = (f32[128,2048]{1,0:T(8,128)}, f32[1,128]{1,0:T(1,128)}) custom-call(s32[1]{0:T(128)} %bitcast.t0_ref, bf16[16384,2048]{1,0:T(8,128)(2,1)} %get-tuple-element.244.a_hbm, bf16[9,48,2048]{2,1,0:T(8,128)(2,1)} %bitcast.28, f32[128,2048]{1,0:T(8,128)} %get-tuple-element.247.st_in, ...), custom_call_target="tpu_custom_call", output_to_operand_aliasing={{0}: (3, {})} | custom-call | tf_op jit(solution)/shard_map/while/body/eval_jaxpr/cond/branch_0_fun/steps_48_1/pallas_call | solution.py:286
  1559.6 3.6 gather_fusion.8
  (60 shorter events, 41.5 us)
Async XLA Ops:
  0.6 14.8 copy-start.3
  0.6 6.8 copy-start.1
  1.5 14.5 copy-start.2
  1559.6 3.6 copy-start
